TPU v7x, 32 devices: a whole 2x2x4 slice. The times are simulated.
32 devices in a mesh: row: 8 (over z, x), col: 4 (over y, core).
Axes of the slice: x: 2, y: 2, z: 4, core: 2. Of those that a mesh axis runs over, the one named last changes fastest.
Arguments:
- snapshot: bfloat16 [512, 256, 512], P('row', 'col'), may hold values from -6 to 6
- basis_two: bfloat16 [256, 128], P('col'), may hold values from -0.375 to 0.375
- basis_three: bfloat16 [512, 128], replicated, may hold values from -0.25 to 0.25
Outputs:
- gram: float32 [512, 512], P('row', 'col')
All inputs are finite; a program needn't handle non-finite values.
Results may differ from a plain program's by a relative error of at most 0.0017.
Values may be sent and summed in bfloat16 or wider, within the bound.
No kernel may reach another device: no remote copies, remote signals or barrier semaphores. Data moves between devices by JAX's collectives and lax.ppermute only.
A program may use at most 64 MiB of HBM per device.

v0:
```python
import jax
import jax.numpy as jnp
from jax import lax
from jax.sharding import PartitionSpec as P


def on_device(snapshot, basis_two, basis_three):
    cells_one, cells_two, cells_three = snapshot.shape
    ranks_two = basis_two.shape[1]
    ranks_three = basis_three.shape[1]
    inner = jnp.dot(
        snapshot.reshape(cells_one * cells_two, cells_three),
        basis_three,
        preferred_element_type=jnp.float32,
    )
    inner = inner.astype(jnp.bfloat16).reshape(cells_one, cells_two, ranks_three)
    regrouped = lax.all_to_all(inner, "col", split_axis=2, concat_axis=1, tiled=True)
    whole_factor = lax.all_gather(basis_two, "col", axis=0, tiled=True)
    full = jnp.einsum("abr,bq->qar", regrouped, whole_factor, preferred_element_type=jnp.float32)
    rounded = lax.all_to_all(
        full.astype(jnp.bfloat16), "col", split_axis=0, concat_axis=2, tiled=True
    )
    partial_gram = jnp.einsum(
        "qar,qbr->ab",
        rounded,
        lax.all_gather(rounded, "row", axis=1, tiled=True),
        preferred_element_type=jnp.float32,
    )
    summed_gram = lax.psum_scatter(partial_gram, "col", scatter_dimension=1, tiled=True)
    return summed_gram * (1.0 / (ranks_two * ranks_three))


def solution(mesh):
    in_specs = (P("row", "col", None), P("col", None), P())
    out_specs = P("row", "col")
    return jax.shard_map(
        on_device, mesh=mesh, in_specs=in_specs, out_specs=out_specs, check_vma=False
    )
```

profile of v0, /device:TPU:0, one launch (start us, length us, event | category | flops | bytes accessed | tf_op | source)
XLA Modules:
  0.0 165.3 jit_solution(16451007527104671222)
XLA Ops:
  6.5 0.0 copy-start
  6.5 0.9 copy-done
  7.4 3.4 %convolution_convert_fusion = bf16[4096,128]{1,0:T(8,128)(2,1)S(1)} fusion(bf16[4096,512]{1,0:T(8,128)(2,1)} %bitcast.31, bf16[512,128]{1,0:T(8,128)(2,1)S(1)} %copy-done), kind=kOutput, calls=%fused_computation | convolution fusion | flops 537395200 | bytes 5373952 | tf_op jit(solution)/shard_map/dot_general | solution.py:11
  10.9 0.0 copy-start.1
  10.9 3.0 %copy.20 = bf16[64,64,128]{1,0,2:T(8,128)(2,1)S(1)} copy(bf16[64,64,128]{2,1,0:T(8,128)(2,1)S(1)} %bitcast.32) | data formatting | bytes 2097152 | tf_op jit(solution)/shard_map/reshape | solution.py:16
  13.9 2.6 %reshape.10 = bf16[4,2,65536]{2,1,0:T(2,128)(2,1)} reshape(bf16[128,64,64]{2,1,0:T(8,128)(2,1)S(1)} %bitcast.29) | data formatting | bytes 2097152
  16.5 4.3 %all-to-all-start = ((bf16[4,2,65536]{2,1,0:T(2,128)(2,1)}), bf16[4,2,65536]{2,1,0:T(2,128)(2,1)S(1)}, u32[]{:S(2)}, u32[]{:S(2)}) async-start(bf16[4,2,65536]{2,1,0:T(2,128)(2,1)} %reshape.10), calls=%async_computation | async-start | bytes 2097152 | tf_op jit(solution)/shard_map/all_to_all | solution.py:17
  20.8 0.0 all-gather.2.cloned.1.call-start
  20.8 0.0 copy-done.1
  20.8 15.6 %all_gather.6 = bf16[256,128]{1,0:T(8,128)(2,1)S(1)} all-gather(bf16[64,128]{1,0:T(8,128)(2,1)S(1)} %copy-done.1), channel_id=1, replica_groups=mesh['row'=8,'col'=4] {'col'}, dimensions={0}, use_global_device_ids=true | all-gather | bytes 81920 | tf_op jit(solution)/shard_map/all_gather | solution.py:18
  36.4 0.0 all-to-all-done
  36.4 1.4 reshape.11
  37.8 3.0 %copy.22 = bf16[64,4,64,32]{2,1,3,0:T(4,128)(2,1)} copy(bf16[64,4,64,32]{2,0,3,1:T(8,128)(2,1)S(1)} %bitcast.30) | data formatting | bytes 2097152 | tf_op jit(solution)/shard_map/all_to_all | solution.py:17
  40.8 3.5 %all_to_all.29 = bf16[64,256,32]{1,2,0:T(8,128)(2,1)S(1)} reshape(bf16[64,4,64,32]{2,1,3,0:T(4,128)(2,1)} %copy.22) | data formatting | bytes 2097152 | tf_op jit(solution)/shard_map/all_to_all | solution.py:17
  44.3 0.4 fusion
  44.7 1.7 %copy.23 = bf16[128,64,32]{1,2,0:T(8,128)(2,1)S(1)} copy(bf16[128,64,32]{0,2,1:T(8,128)(2,1)S(1)} %fusion) | data formatting | bytes 1048576 | tf_op jit(solution)/shard_map/convert_element_type | solution.py:21
  46.4 0.9 reshape.12
  47.3 11.2 %all_to_all.36 = bf16[4,2,32768]{2,1,0:T(2,128)(2,1)S(1)} all-to-all(bf16[4,2,32768]{2,1,0:T(2,128)(2,1)S(1)} %reshape.12), channel_id=1, replica_groups=mesh['row'=8,'col'=4] {'col'}, dimensions={0} | all-to-all | bytes 1048576 | tf_op jit(solution)/shard_map/all_to_all | solution.py:20
  58.5 0.7 reshape.13
  59.2 0.1 copy.24
  59.4 1.1 copy.25
  60.5 0.0 all-gather.2.cloned.1.call-update
  60.5 0.0 reduce-scatter.2.cloned.1.call-start
  60.6 73.9 %all-gather.2.cloned.1.call-done = bf16[32,512,128]{2,1,0:T(8,128)(2,1)} async-done(((bf16[32,64,128]{2,1,0:T(8,128)(2,1)}), bf16[32,512,128]{2,1,0:T(8,128)(2,1)}) %all-gather.2.cloned.1.call-update) | async-done | bytes 4194320 | tf_op jit(solution)/shard_map/all_gather | solution.py:26
  134.4 4.2 %convolution_bitcast_fusion = f32[64,512]{1,0:T(8,128)} fusion(bf16[32,64,128]{1,2,0:T(8,128)(2,1)S(1)} %bitcast.28, bf16[32,512,128]{2,1,0:T(8,128)(2,1)} %all-gather.2.cloned.1.call-done), kind=kOutput, calls=%fused_computation.3 | convolution fusion | flops 268435456 | bytes 4849664 | tf_op jit(solution)/shard_map/qar,qbr->ab/dot_general | solution.py:23
  138.7 0.0 reduce-scatter.2.cloned.1.call-update
  138.7 18.3 %reduce-scatter.2.cloned.1.call-done = f32[64,128]{1,0:T(8,128)} async-done(((f32[64,512]{1,0:T(8,128)}), f32[64,128]{1,0:T(8,128)}) %reduce-scatter.2.cloned.1.call-update) | async-done | bytes 32784 | tf_op jit(solution)/shard_map/reduce_scatter | solution.py:29
  157.0 1.4 broadcast_multiply_fusion
Async XLA Ops:
  6.5 0.9 copy-start
  10.9 9.9 %copy-start.1 = (bf16[64,128]{1,0:T(8,128)(2,1)S(1)}, bf16[64,128]{1,0:T(8,128)(2,1)}, u32[]{:S(2)}) copy-start(bf16[64,128]{1,0:T(8,128)(2,1)} %param.4) | copy-start | bytes 49156
  16.5 19.9 %all-to-all-start = ((bf16[4,2,65536]{2,1,0:T(2,128)(2,1)}), bf16[4,2,65536]{2,1,0:T(2,128)(2,1)S(1)}, u32[]{:S(2)}, u32[]{:S(2)}) async-start(bf16[4,2,65536]{2,1,0:T(2,128)(2,1)} %reshape.10), calls=%async_computation | async-start | bytes 2097152 | tf_op jit(solution)/shard_map/all_to_all | solution.py:17
  20.8 113.7 %all-gather.2.cloned.1.call-start = ((), (), s32[]{:S(2)}) async-start(), calls=%async_computation.3 | async-start | bytes 4718592 | tf_op jit(solution)/shard_map/all_gather | solution.py:26
  60.5 96.5 %reduce-scatter.2.cloned.1.call-start = ((), (), s32[]{:S(2)}) async-start(), calls=%async_computation.4 | async-start | bytes 163840 | tf_op jit(solution)/shard_map/reduce_scatter | solution.py:29
Sparse Core Ops, SparseCore 0:
  60.6 73.7 all-gather.1
  138.8 18.1 reduce-scatter.1
where the time goes:
time: 166 us; the launch traced here: 165 us
  waiting for transfers between devices  92.3 us (56%)
  blocking collectives  26.8 us (16%)
  local copies, waits for them, and re-layouts  18.9 us (11%)
  between operations  13.5 us (8%)
  matrix products  8.09 us (5%)
  starting transfers between devices  4.3 us (3%)
    all_gather x1, waiting for transfers between devices, on_device(): lax.all_gather(rounded, 'row', axis=1, tiled=True)  73.9 us
    reduce_scatter x1, waiting for transfers between devices, on_device(): lax.psum_scatter(partial_gram, 'col', scatter_dimension=1, tiled=True)  18.3 us
    all_gather x1, blocking collectives, on_device(): whole_factor = lax.all_gather(basis_two, 'col', axis=0, tiled=True)  15.6 us
    all_to_all x1, blocking collectives, on_device(): lax.all_to_all(full.astype(jnp.bfloat16), 'col', split_axis=0, concat_axi...  11.2 us
    unnamed x8, local copies, waits for them, and re-layouts  6.55 us
    all_to_all x2, local copies, waits for them, and re-layouts, on_device(): lax.all_to_all(inner, 'col', split_axis=2, concat_axis=1, tiled=True)  6.45 us
    all_to_all x1, starting transfers between devices, on_device(): lax.all_to_all(inner, 'col', split_axis=2, concat_axis=1, tiled=True)  4.26 us
    dot_general x1, matrix products, on_device(): jnp.einsum('qar,qbr->ab', rounded, lax.all_gather(rounded, 'row', axis=1,...  4.22 us
  transfers between devices with their start and end apart: 3, of which 2 were waited for; matrix products, arithmetic and copies ran while one was open for 0% of the time, Pallas kernels for 0%

commit v1 on v0

--- a/solution.py
+++ b/solution.py
@@ -2,6 +2,13 @@
 import jax.numpy as jnp
 from jax import lax
 from jax.sharding import PartitionSpec as P
+
+
+def raise_leaf(array_in, ndim_at):
+    carry_in = list(array_in.shape[1:])
+    carry_in[ndim_at] *= array_in.shape[0]
+    current_arr = jnp.moveaxis(array_in, 0, ndim_at).reshape(carry_in)
+    return current_arr
 
 
 def on_device(snapshot, basis_two, basis_three):
@@ -20,11 +27,44 @@
     rounded = lax.all_to_all(
         full.astype(jnp.bfloat16), "col", split_axis=0, concat_axis=2, tiled=True
     )
-    partial_gram = jnp.einsum(
-        "qar,qbr->ab",
+
+    def show_limits(sample, group_axis, pos_dim, xs, dim_i):
+        y1 = lax.axis_size(group_axis)
+        t_next = lax.axis_index(group_axis)
+        m_next, vec_out, side_arr = (y1, t_next, sample.shape[pos_dim])
+        pool = [(dd, (dd + 1) % m_next) for dd in range(m_next)]
+        by_place = [(dd, (dd - 1) % m_next) for dd in range(m_next)]
+        taken_in = m_next // 2
+        built = {}
+        field_out = v_next = sample
+        for src_i in range(taken_in + 1):
+            right_arr = (
+                lax.ppermute(field_out, axis_name=group_axis, perm=pool)
+                if src_i < taken_in
+                else None
+            )
+            found_now = (
+                lax.ppermute(v_next, axis_name=group_axis, perm=by_place)
+                if src_i < m_next - taken_in - 1
+                else None
+            )
+            built[-src_i] = xs(field_out, (vec_out - src_i) % m_next * side_arr)
+            if 0 < src_i < m_next - taken_in:
+                built[src_i] = xs(v_next, (vec_out + src_i) % m_next * side_arr)
+            field_out, v_next = (right_arr, found_now)
+        built = jnp.stack([built[i0] for i0 in sorted(built)], axis=0)
+        built = built[(jnp.arange(m_next) - vec_out + taken_in) % m_next]
+        now = raise_leaf(built, dim_i)
+        return now
+
+    partial_gram = show_limits(
         rounded,
-        lax.all_gather(rounded, "row", axis=1, tiled=True),
-        preferred_element_type=jnp.float32,
+        "row",
+        1,
+        lambda own_block, at: jnp.einsum(
+            "qar,qbr->ab", rounded, own_block, preferred_element_type=jnp.float32
+        ),
+        1,
     )
     summed_gram = lax.psum_scatter(partial_gram, "col", scatter_dimension=1, tiled=True)
     return summed_gram * (1.0 / (ranks_two * ranks_three))

time: 166 us -> 183 us (1.10)
  starting transfers between devices: 4.3 us -> 42.2 us
  waiting for transfers between devices: 92.3 us -> 66.9 us
  matrix products: 8.09 us -> 11.8 us
    all_gather x1 -> x0, waiting for transfers between devices: 73.9 us -> none  [on_device(): lax.all_gather(rounded, 'row', axis=1, tiled=True)]
    ppermute x0 -> x7, waiting for transfers between devices: none -> 48.1 us  [the longest x4 48.1 us: show_limits(): lax.ppermute(field_out, axis_name=group_axis, perm=pool)]
    ppermute x0 -> x7, starting transfers between devices: none -> 38 us  [the longest x3 30.7 us: show_limits(): lax.ppermute(v_next, axis_name=group_axis, perm=by_place)]
    dot_general x1 -> x8, matrix products: 4.22 us -> 7.99 us  [on_device(): jnp.einsum('qar,qbr->ab', rounded, own_block, preferred_element_type=jnp....]
    unnamed x8 -> x12, local copies, waits for them, and re-layouts: 6.55 us -> 6.57 us
  transfers between devices with their start and end apart: 3 -> 9, of which waited for: 2 -> 5; matrix products, arithmetic and copies ran while one was open for 0% -> 4% of each run, Pallas kernels for 0% -> 0%
where the time goes in v1:
time: 183 us; the launch traced here: 182 us
  waiting for transfers between devices  66.9 us (37%)
  starting transfers between devices  42.2 us (23%)
  blocking collectives  26.8 us (15%)
  local copies, waits for them, and re-layouts  19.7 us (11%)
  between operations  13.6 us (7%)
  matrix products  11.8 us (6%)
    ppermute x4, waiting for transfers between devices, show_limits(): lax.ppermute(field_out, axis_name=group_axis, perm=pool)  48.1 us
    ppermute x3, starting transfers between devices, show_limits(): lax.ppermute(v_next, axis_name=group_axis, perm=by_place)  30.7 us
    reduce_scatter x1, waiting for transfers between devices, on_device(): lax.psum_scatter(partial_gram, 'col', scatter_dimension=1, tiled=True)  18.9 us
    all_gather x1, blocking collectives, on_device(): whole_factor = lax.all_gather(basis_two, 'col', axis=0, tiled=True)  15.6 us
    all_to_all x1, blocking collectives, on_device(): lax.all_to_all(full.astype(jnp.bfloat16), 'col', split_axis=0, concat_axi...  11.2 us
    dot_general x8, matrix products, on_device(): jnp.einsum('qar,qbr->ab', rounded, own_block, preferred_element_type=jnp....  7.99 us
    ppermute x4, starting transfers between devices, show_limits(): lax.ppermute(field_out, axis_name=group_axis, perm=pool)  7.31 us
    unnamed x12, local copies, waits for them, and re-layouts  6.57 us
  transfers between devices with their start and end apart: 9, of which 5 were waited for; matrix products, arithmetic and copies ran while one was open for 4% of the time, Pallas kernels for 0%

profile of v1, /device:TPU:0, one launch (start us, length us, event | category | flops | bytes accessed | tf_op | source)
XLA Modules:
  0.0 182.5 jit_solution(4565947094073385699)
XLA Ops:
  6.5 0.0 copy-start
  6.5 0.9 copy-done
  7.4 3.4 %convolution_convert_fusion = bf16[4096,128]{1,0:T(8,128)(2,1)S(1)} fusion(bf16[4096,512]{1,0:T(8,128)(2,1)} %bitcast.95, bf16[512,128]{1,0:T(8,128)(2,1)S(1)} %copy-done), kind=kOutput, calls=%fused_computation.1 | convolution fusion | flops 537395200 | bytes 5373952 | tf_op jit(solution)/shard_map/dot_general | solution.py:18
  10.9 0.0 copy-start.3
  10.9 3.0 %copy.37 = bf16[64,64,128]{1,0,2:T(8,128)(2,1)S(1)} copy(bf16[64,64,128]{2,1,0:T(8,128)(2,1)S(1)} %bitcast.96) | data formatting | bytes 2097152 | tf_op jit(solution)/shard_map/reshape | solution.py:23
  13.9 2.7 %reshape.81 = bf16[4,2,65536]{2,1,0:T(2,128)(2,1)} reshape(bf16[128,64,64]{2,1,0:T(8,128)(2,1)S(1)} %bitcast.93) | data formatting | bytes 2097152
  16.5 4.3 %all-to-all-start = ((bf16[4,2,65536]{2,1,0:T(2,128)(2,1)}), bf16[4,2,65536]{2,1,0:T(2,128)(2,1)S(1)}, u32[]{:S(2)}, u32[]{:S(2)}) async-start(bf16[4,2,65536]{2,1,0:T(2,128)(2,1)} %reshape.81), calls=%async_computation | async-start | bytes 2097152 | tf_op jit(solution)/shard_map/all_to_all | solution.py:24
  20.8 0.0 reduce-scatter.2.cloned.1.call-start
  20.8 0.0 copy-done.3
  20.8 15.6 %all_gather.3 = bf16[256,128]{1,0:T(8,128)(2,1)S(1)} all-gather(bf16[64,128]{1,0:T(8,128)(2,1)S(1)} %copy-done.3), channel_id=1, replica_groups=mesh['row'=8,'col'=4] {'col'}, dimensions={0}, use_global_device_ids=true | all-gather | bytes 81920 | tf_op jit(solution)/shard_map/all_gather | solution.py:25
  36.4 0.0 all-to-all-done
  36.4 1.4 reshape.82
  37.9 2.9 %copy.39 = bf16[64,4,64,32]{2,1,3,0:T(4,128)(2,1)} copy(bf16[64,4,64,32]{2,0,3,1:T(8,128)(2,1)S(1)} %bitcast.94) | data formatting | bytes 2097152 | tf_op jit(solution)/shard_map/all_to_all | solution.py:24
  40.8 3.5 %all_to_all.29 = bf16[64,256,32]{1,2,0:T(8,128)(2,1)S(1)} reshape(bf16[64,4,64,32]{2,1,3,0:T(4,128)(2,1)} %copy.39) | data formatting | bytes 2097152 | tf_op jit(solution)/shard_map/all_to_all | solution.py:24
  44.3 0.4 fusion
  44.7 1.7 copy.40
  46.4 0.9 reshape.83
  47.3 11.2 %all_to_all.36 = bf16[4,2,32768]{2,1,0:T(2,128)(2,1)S(1)} all-to-all(bf16[4,2,32768]{2,1,0:T(2,128)(2,1)S(1)} %reshape.83), channel_id=1, replica_groups=mesh['row'=8,'col'=4] {'col'}, dimensions={0} | all-to-all | bytes 1048576 | tf_op jit(solution)/shard_map/all_to_all | solution.py:27
  58.5 0.7 reshape.84
  59.2 0.1 copy.41
  59.4 0.4 copy.42
  59.8 0.0 copy-start.2
  59.8 2.2 %collective-permute-start = (bf16[32,64,128]{2,1,0:T(8,128)(2,1)S(1)}, bf16[32,64,128]{2,1,0:T(8,128)(2,1)S(1)}, u32[]{:S(2)}, u32[]{:S(2)}) collective-permute-start(bf16[32,64,128]{2,1,0:T(8,128)(2,1)S(1)} %copy.42), channel_id=1, source_target_pairs={{0,4},{4,8},{8,12},{12,16},{16,20},{20,24},{24,28},{28,0},{1,5},{5... | collective-permute-start | bytes 1572872 | tf_op jit(solution)/shard_map/ppermute | solution.py:42
  62.0 14.6 %collective-permute-done = bf16[32,64,128]{2,1,0:T(8,128)(2,1)S(1)} collective-permute-done((bf16[32,64,128]{2,1,0:T(8,128)(2,1)S(1)}, bf16[32,64,128]{2,1,0:T(8,128)(2,1)S(1)}, u32[]{:S(2)}, u32[]{:S(2)}) %collective-permute-start) | collective-permute-done | bytes 524320 | tf_op jit(solution)/shard_map/ppermute | solution.py:42
  76.6 0.0 copy-done.2
  76.6 0.0 collective-permute-start.1
  76.6 4.7 %collective-permute-start.4 = (bf16[32,64,128]{2,1,0:T(8,128)(2,1)}, bf16[32,64,128]{2,1,0:T(8,128)(2,1)S(1)}, u32[]{:S(2)}, u32[]{:S(2)}) collective-permute-start(bf16[32,64,128]{2,1,0:T(8,128)(2,1)} %copy-done.2), channel_id=1, source_target_pairs={{0,28},{4,0},{8,4},{12,8},{16,12},{20,16},{24,20},{28,24},{1,29},{... | collective-permute-start | bytes 1572872 | tf_op jit(solution)/shard_map/ppermute | solution.py:47
  81.3 17.0 %collective-permute-done.1 = bf16[32,64,128]{2,1,0:T(8,128)(2,1)S(1)} collective-permute-done((bf16[32,64,128]{2,1,0:T(8,128)(2,1)S(1)}, bf16[32,64,128]{2,1,0:T(8,128)(2,1)S(1)}, u32[]{:S(2)}, u32[]{:S(2)}) %collective-permute-start.1) | collective-permute-done | bytes 524320 | tf_op jit(solution)/shard_map/ppermute | solution.py:42
  98.4 0.0 copy-start.1
  98.4 2.5 %collective-permute-start.2 = (bf16[32,64,128]{2,1,0:T(8,128)(2,1)S(1)}, bf16[32,64,128]{2,1,0:T(8,128)(2,1)}, u32[]{:S(2)}, u32[]{:S(2)}) collective-permute-start(bf16[32,64,128]{2,1,0:T(8,128)(2,1)S(1)} %collective-permute-done.1), channel_id=1, source_target_pairs={{0,4},{4,8},{8,12},{12,16},{16,20},{20,24},{24,28},{28,0},{1,5},{5... | collective-permute-start | bytes 1572872 | tf_op jit(solution)/shard_map/ppermute | solution.py:42
  100.8 0.0 collective-permute-done.4
  100.9 0.0 copy-done.1
  100.9 12.4 %collective-permute-start.5 = (bf16[32,64,128]{2,1,0:T(8,128)(2,1)S(1)}, bf16[32,64,128]{2,1,0:T(8,128)(2,1)}, u32[]{:S(2)}, u32[]{:S(2)}) collective-permute-start(bf16[32,64,128]{2,1,0:T(8,128)(2,1)S(1)} %collective-permute-done.4), channel_id=1, source_target_pairs={{0,28},{4,0},{8,4},{12,8},{16,12},{20,16},{24,20},{28,24},{1,29},{... | collective-permute-start | bytes 1572872 | tf_op jit(solution)/shard_map/ppermute | solution.py:47
  113.2 8.8 %collective-permute-done.2 = bf16[32,64,128]{2,1,0:T(8,128)(2,1)} collective-permute-done((bf16[32,64,128]{2,1,0:T(8,128)(2,1)S(1)}, bf16[32,64,128]{2,1,0:T(8,128)(2,1)}, u32[]{:S(2)}, u32[]{:S(2)}) %collective-permute-start.2) | collective-permute-done | bytes 524320 | tf_op jit(solution)/shard_map/ppermute | solution.py:42
  122.0 2.6 %collective-permute-start.3 = (bf16[32,64,128]{2,1,0:T(8,128)(2,1)}, bf16[32,64,128]{2,1,0:T(8,128)(2,1)}, u32[]{:S(2)}, u32[]{:S(2)}) collective-permute-start(bf16[32,64,128]{2,1,0:T(8,128)(2,1)} %collective-permute-done.2), channel_id=1, source_target_pairs={{0,4},{4,8},{8,12},{12,16},{16,20},{20,24},{24,28},{28,0},{1,5},{5... | collective-permute-start | bytes 1572872 | tf_op jit(solution)/shard_map/ppermute | solution.py:42
  124.6 0.0 collective-permute-done.5
  124.7 13.6 %collective-permute-start.6 = (bf16[32,64,128]{2,1,0:T(8,128)(2,1)}, bf16[32,64,128]{2,1,0:T(8,128)(2,1)S(1)}, u32[]{:S(2)}, u32[]{:S(2)}) collective-permute-start(bf16[32,64,128]{2,1,0:T(8,128)(2,1)} %collective-permute-done.5), channel_id=1, source_target_pairs={{0,28},{4,0},{8,4},{12,8},{16,12},{20,16},{24,20},{28,24},{1,29},{... | collective-permute-start | bytes 1572872 | tf_op jit(solution)/shard_map/ppermute | solution.py:47
  138.2 7.6 %collective-permute-done.3 = bf16[32,64,128]{2,1,0:T(8,128)(2,1)} collective-permute-done((bf16[32,64,128]{2,1,0:T(8,128)(2,1)}, bf16[32,64,128]{2,1,0:T(8,128)(2,1)}, u32[]{:S(2)}, u32[]{:S(2)}) %collective-permute-start.3) | collective-permute-done | bytes 524320 | tf_op jit(solution)/shard_map/ppermute | solution.py:42
  145.8 1.5 fusion.7
  147.3 1.5 fusion.6
  148.8 1.5 fusion.5
  150.4 0.5 fusion.4
  150.9 0.4 fusion.8
  151.3 0.5 fusion.3
  151.8 1.5 fusion.2
  153.4 0.0 collective-permute-done.6
  153.4 0.5 fusion.1
  153.9 0.6 gather_fusion
  154.5 0.2 copy.51
  154.6 0.8 reshape.63
  155.4 0.0 reduce-scatter.2.cloned.1.call-update
  155.4 18.9 %reduce-scatter.2.cloned.1.call-done = f32[64,128]{1,0:T(8,128)} async-done(((f32[64,512]{1,0:T(8,128)}), f32[64,128]{1,0:T(8,128)}) %reduce-scatter.2.cloned.1.call-update) | async-done | bytes 32784 | tf_op jit(solution)/shard_map/reduce_scatter | solution.py:69
  174.3 1.4 broadcast_multiply_fusion
  (2 shorter events, 0.0 us)
Async XLA Ops:
  6.5 0.9 copy-start
  10.9 9.9 %copy-start.3 = (bf16[64,128]{1,0:T(8,128)(2,1)S(1)}, bf16[64,128]{1,0:T(8,128)(2,1)}, u32[]{:S(2)}) copy-start(bf16[64,128]{1,0:T(8,128)(2,1)} %param.4) | copy-start | bytes 49156
  16.5 19.9 %all-to-all-start = ((bf16[4,2,65536]{2,1,0:T(2,128)(2,1)}), bf16[4,2,65536]{2,1,0:T(2,128)(2,1)S(1)}, u32[]{:S(2)}, u32[]{:S(2)}) async-start(bf16[4,2,65536]{2,1,0:T(2,128)(2,1)} %reshape.81), calls=%async_computation | async-start | bytes 2097152 | tf_op jit(solution)/shard_map/all_to_all | solution.py:24
  20.8 153.4 %reduce-scatter.2.cloned.1.call-start = ((), (), s32[]{:S(2)}) async-start(), calls=%async_computation.3 | async-start | bytes 163840 | tf_op jit(solution)/shard_map/reduce_scatter | solution.py:69
  59.8 16.8 %copy-start.2 = (bf16[32,64,128]{2,1,0:T(8,128)(2,1)}, bf16[32,64,128]{2,1,0:T(8,128)(2,1)S(1)}, u32[]{:S(2)}) copy-start(bf16[32,64,128]{2,1,0:T(8,128)(2,1)S(1)} %copy.42) | copy-start | bytes 1572868
  59.8 16.8 %collective-permute-start = (bf16[32,64,128]{2,1,0:T(8,128)(2,1)S(1)}, bf16[32,64,128]{2,1,0:T(8,128)(2,1)S(1)}, u32[]{:S(2)}, u32[]{:S(2)}) collective-permute-start(bf16[32,64,128]{2,1,0:T(8,128)(2,1)S(1)} %copy.42), channel_id=1, source_target_pairs={{0,4},{4,8},{8,12},{12,16},{16,20},{20,24},{24,28},{28,0},{1,5},{5... | collective-permute-start | bytes 1572872 | tf_op jit(solution)/shard_map/ppermute | solution.py:42
  76.6 21.8 %collective-permute-start.1 = (bf16[32,64,128]{2,1,0:T(8,128)(2,1)S(1)}, bf16[32,64,128]{2,1,0:T(8,128)(2,1)S(1)}, u32[]{:S(2)}, u32[]{:S(2)}) collective-permute-start(bf16[32,64,128]{2,1,0:T(8,128)(2,1)S(1)} %collective-permute-done), channel_id=1, source_target_pairs={{0,4},{4,8},{8,12},{12,16},{16,20},{20,24},{24,28},{28,0},{1,5},{5... | collective-permute-start | bytes 1572872 | tf_op jit(solution)/shard_map/ppermute | solution.py:42
  76.6 24.2 %collective-permute-start.4 = (bf16[32,64,128]{2,1,0:T(8,128)(2,1)}, bf16[32,64,128]{2,1,0:T(8,128)(2,1)S(1)}, u32[]{:S(2)}, u32[]{:S(2)}) collective-permute-start(bf16[32,64,128]{2,1,0:T(8,128)(2,1)} %copy-done.2), channel_id=1, source_target_pairs={{0,28},{4,0},{8,4},{12,8},{16,12},{20,16},{24,20},{28,24},{1,29},{... | collective-permute-start | bytes 1572872 | tf_op jit(solution)/shard_map/ppermute | solution.py:47
  98.4 2.5 %copy-start.1 = (bf16[32,64,128]{2,1,0:T(8,128)(2,1)}, bf16[32,64,128]{2,1,0:T(8,128)(2,1)S(1)}, u32[]{:S(2)}) copy-start(bf16[32,64,128]{2,1,0:T(8,128)(2,1)S(1)} %collective-permute-done.1) | copy-start | bytes 1572868
  98.4 23.7 %collective-permute-start.2 = (bf16[32,64,128]{2,1,0:T(8,128)(2,1)S(1)}, bf16[32,64,128]{2,1,0:T(8,128)(2,1)}, u32[]{:S(2)}, u32[]{:S(2)}) collective-permute-start(bf16[32,64,128]{2,1,0:T(8,128)(2,1)S(1)} %collective-permute-done.1), channel_id=1, source_target_pairs={{0,4},{4,8},{8,12},{12,16},{16,20},{20,24},{24,28},{28,0},{1,5},{5... | collective-permute-start | bytes 1572872 | tf_op jit(solution)/shard_map/ppermute | solution.py:42
  100.9 23.8 %collective-permute-start.5 = (bf16[32,64,128]{2,1,0:T(8,128)(2,1)S(1)}, bf16[32,64,128]{2,1,0:T(8,128)(2,1)}, u32[]{:S(2)}, u32[]{:S(2)}) collective-permute-start(bf16[32,64,128]{2,1,0:T(8,128)(2,1)S(1)} %collective-permute-done.4), channel_id=1, source_target_pairs={{0,28},{4,0},{8,4},{12,8},{16,12},{20,16},{24,20},{28,24},{1,29},{... | collective-permute-start | bytes 1572872 | tf_op jit(solution)/shard_map/ppermute | solution.py:47
  122.0 23.8 %collective-permute-start.3 = (bf16[32,64,128]{2,1,0:T(8,128)(2,1)}, bf16[32,64,128]{2,1,0:T(8,128)(2,1)}, u32[]{:S(2)}, u32[]{:S(2)}) collective-permute-start(bf16[32,64,128]{2,1,0:T(8,128)(2,1)} %collective-permute-done.2), channel_id=1, source_target_pairs={{0,4},{4,8},{8,12},{12,16},{16,20},{20,24},{24,28},{28,0},{1,5},{5... | collective-permute-start | bytes 1572872 | tf_op jit(solution)/shard_map/ppermute | solution.py:42
  124.7 28.7 %collective-permute-start.6 = (bf16[32,64,128]{2,1,0:T(8,128)(2,1)}, bf16[32,64,128]{2,1,0:T(8,128)(2,1)S(1)}, u32[]{:S(2)}, u32[]{:S(2)}) collective-permute-start(bf16[32,64,128]{2,1,0:T(8,128)(2,1)} %collective-permute-done.5), channel_id=1, source_target_pairs={{0,28},{4,0},{8,4},{12,8},{16,12},{20,16},{24,20},{28,24},{1,29},{... | collective-permute-start | bytes 1572872 | tf_op jit(solution)/shard_map/ppermute | solution.py:47
Sparse Core Ops, SparseCore 0:
  155.5 18.6 reduce-scatter.1
